TPU v7x, 128 devices: a whole 4x4x4 slice. The times are simulated.
128 devices in a mesh: rows: 16 (over y, z), trees: 8 (over x, core).
Axes of the slice: x: 4, y: 4, z: 4, core: 2. Of those that a mesh axis runs over, the one named last changes fastest.
Arguments:
- leaf_index: int32 [128, 262144], P(None, ('rows', 'trees')), may hold values from 0 to 31, as said below
- out_of_bag: bfloat16 [128, 262144], P(None, ('rows', 'trees')), may hold values from 0 to 4, as said below
- labels: int32 [262144], P(('rows', 'trees')), may hold values from 0 to 999
Outputs:
- tallies: float32 [128, 32, 1000], P('trees', 'rows')
- tree_error: float32 [128], P('trees')
- forest_error: float32 [], replicated
Inputs may be any that keep to these rules, and one draw needn't show every extreme that they name: `out_of_bag`: 0 exactly where a row was in a tree's sample, else at least 0.25. `leaf_index`: in each tree, the 2048 rows of one device reach every leaf exactly 2048 // 32 times.
All inputs are finite; a program needn't handle non-finite values.
Results may differ from a plain program's by a relative error of at most 0.0003.
Values sent between devices are 32-bit elements; how exact they have to be, the bound alone decides.
No kernel may reach another device: no remote copies, remote signals or barrier semaphores. Data moves between devices by JAX's collectives and lax.ppermute only.
A program may use at most 128 MiB of HBM per device.

v0:
```python
import jax
import jax.numpy as jnp
from jax import lax
from jax.sharding import Mesh
from jax.sharding import PartitionSpec as P

CLASSES = 1000
LEAVES = 32
ROWS = ("rows_0", "rows_1")
TREES = ("trees_0", "trees_1")
ROWS_TREES = ("rows_0", "rows_1", "trees_0", "trees_1")


def in_blocks(shard, dim, peers):
    before, after = (shard.shape[:dim], shard.shape[dim + 1 :])
    return jnp.moveaxis(shard.reshape(*before, peers, -1, *after), dim, 0)


def summed_on_arrival(shard, axis, dim):
    peers = lax.axis_size(axis)
    parts = lax.all_to_all(in_blocks(shard, dim, peers), axis, 0, 0, tiled=True)
    return jnp.sum(parts, axis=0)


def by_axis(shard, axes):
    for axis in axes:
        shard = lax.psum(shard, axis)
    return shard


def count_table(leaves, weights, row_labels, n_rows):
    leaf_block_size = LEAVES // n_rows
    leaf_grid = jnp.arange(LEAVES, dtype=jnp.int32).reshape(n_rows, leaf_block_size)
    class_ids = jnp.arange(CLASSES, dtype=jnp.int32)
    class_onehot = (row_labels[:, None] == class_ids[None, :]).astype(jnp.bfloat16)
    placed = jnp.where(
        leaves[None, :, None, :] == leaf_grid[:, None, :, None],
        weights[None, :, None, :],
        jnp.zeros((), jnp.bfloat16),
    )
    count_grid = jnp.einsum(
        "rtlz,zc->rtlc", placed, class_onehot, preferred_element_type=jnp.float32
    )
    return count_grid.reshape(-1, CLASSES)


def per_device(leaf_index, out_of_bag, labels):
    n_rows = lax.axis_size(ROWS)
    tree_count = lax.axis_size(TREES)
    tree_block = leaf_index.shape[0] // tree_count
    leaf_block_slice = LEAVES // n_rows
    ordered = count_table(leaf_index, out_of_bag, labels, n_rows)
    partial_sum_table = lax.psum_scatter(ordered, ROWS, scatter_dimension=0, tiled=True)
    owned_part = summed_on_arrival(partial_sum_table, TREES, 0)
    tallies = owned_part.reshape(tree_block, leaf_block_slice, CLASSES)
    leaf_total = jnp.sum(tallies, axis=2)
    leaf_top = jnp.max(tallies, axis=2)
    local_wrong = jnp.sum(leaf_total - leaf_top, axis=1)
    local_seen = jnp.sum(leaf_total, axis=1)
    wrong_sum, seen_sum = (by_axis(local_wrong, ROWS), by_axis(local_seen, ROWS))
    tree_error = wrong_sum / seen_sum
    all_wrong, all_seen = (
        by_axis(jnp.sum(local_wrong), ROWS_TREES),
        by_axis(jnp.sum(local_seen), ROWS_TREES),
    )
    forest_error = all_wrong / all_seen
    return (tallies, tree_error, forest_error)


def solution(mesh):
    split = Mesh(mesh.devices.reshape(4, 4, 4, 2), ("rows_0", "rows_1", "trees_0", "trees_1"))
    placed = (P(None, ROWS_TREES), P(None, ROWS_TREES), P(ROWS_TREES))
    return jax.shard_map(
        per_device,
        mesh=split,
        in_specs=placed,
        out_specs=(P(TREES, ROWS, None), P(TREES), P()),
        check_vma=False,
    )
```

profile of v0, /device:TPU:1, one launch (start us, length us, event | category | flops | bytes accessed | tf_op | source)
XLA Modules:
  0.0 254.7 jit_solution(17443909807189443048)
XLA Ops:
  7.2 0.0 reduce-scatter.2.cloned.1.call-start
  7.2 21.7 %fusion = f32[16,128,2,1000]{1,3,2,0:T(8,128)} fusion(s32[16,2]{1,0:T(8,128)S(1)} %multiply_add_fusion, s32[128,2048]{1,0:T(8,128)} %param.3, bf16[128,2048]{1,0:T(8,128)(2,1)} %param.4, s32[2048]{0:T(1024)} %param.5), kind=kOutput, calls=%fused_computation.1 | convolution fusion | flops 16796041216 | bytes 17965184 | tf_op jit(solution)/shard_map/rtlz,zc->rtlc/dot_general | solution.py:41
  29.0 25.1 %copy.6 = f32[16,128,2,1000]{3,2,1,0:T(2,128)} copy(f32[16,128,2,1000]{1,3,2,0:T(8,128)} %fusion) | data formatting | bytes 32768000 | tf_op jit(solution)/shard_map/rtlz,zc->rtlc/dot_general | solution.py:41
  54.0 20.8 %reshape.34 = f32[4096,1000]{1,0:T(8,128)} reshape(f32[16,128,2,1000]{3,2,1,0:T(2,128)} %copy.6) | data formatting | bytes 32768000 | tf_op jit(solution)/shard_map/reshape | solution.py:44
  74.8 0.0 reduce-scatter.2.cloned.1.call-update
  74.8 114.0 %reduce-scatter.2.cloned.1.call-done = f32[256,1000]{1,0:T(8,128)} async-done(((f32[4096,1000]{1,0:T(8,128)}), f32[256,1000]{1,0:T(8,128)}) %reduce-scatter.2.cloned.1.call-update) | async-done | bytes 1024016 | tf_op jit(solution)/shard_map/reduce_scatter | solution.py:53
  188.9 20.1 %all_to_all.5 = f32[8,32,1000]{2,1,0:T(8,128)S(1)} all-to-all(f32[8,32,1000]{2,1,0:T(8,128)} %bitcast.6), channel_id=1, replica_groups=mesh['rows_0'=4,'rows_1'=4,'trees_0'=4,'trees_1'=2] {'trees_0','trees_1'}, dimensions={0} | all-to-all | bytes 2048000 | tf_op jit(solution)/shard_map/all_to_all | solution.py:21
  209.0 0.9 fusion.9
  209.9 0.7 reshape.36
  210.6 0.1 reduce_max.11
  210.7 0.1 reduce_max.12
  210.8 0.6 subtract_reduce_fusion.1
  211.4 0.1 reduce_sum.58
  211.5 0.1 fusion.10
  211.6 8.7 %all-reduce.2 = (f32[16]{0:T(128)S(1)}, f32[16]{0:T(128)S(1)}, f32[]{:T(128)}, f32[]{:T(128)}) all-reduce(f32[16]{0:T(128)S(1)} %get-tuple-element.7, f32[16]{0:T(128)S(1)} %get-tuple-element.6, f32[]{:T(128)} %subtract_reduce_fusion.1, f32[]{:T(128)} %get-tuple-element.3), channel_id=1, replica_groups=mesh['rows_0'=4,'rows_1'=4,'trees_0'=4,'trees_1'=2] {'rows_0'}, use_global_device_ids=true, to_apply=%region_5.6 | all-reduce | flops 34 | bytes 272 | tf_op jit(solution)/shard_map/psum | solution.py:27
  220.3 7.4 %all-reduce.1 = (f32[16]{0:T(128)S(1)}, f32[16]{0:T(128)S(1)}, f32[]{:T(128)}, f32[]{:T(128)}) all-reduce(f32[16]{0:T(128)S(1)} %get-tuple-element.14, f32[16]{0:T(128)S(1)} %get-tuple-element.15, f32[]{:T(128)} %get-tuple-element.16, f32[]{:T(128)} %get-tuple-element.17), channel_id=1, replica_groups=mesh['rows_0'=4,'rows_1'=4,'trees_0'=4,'trees_1'=2] {'rows_1'}, use_global_device_ids=true, to_apply=%region_6.7 | all-reduce | flops 34 | bytes 272 | tf_op jit(solution)/shard_map/psum | solution.py:27
  227.7 0.5 div.6
  228.2 7.6 %all-reduce = (f32[]{:T(128)}, f32[]{:T(128)}) all-reduce(f32[]{:T(128)} %get-tuple-element.12, f32[]{:T(128)} %get-tuple-element.13), channel_id=1, replica_groups=mesh['rows_0'=4,'rows_1'=4,'trees_0'=4,'trees_1'=2] {'trees_0'}, use_global_device_ids=true, to_apply=%region_13.14 | all-reduce | flops 2 | bytes 16 | tf_op jit(solution)/shard_map/psum | solution.py:27
  235.8 9.7 %all-reduce.3 = (f32[]{:T(128)}, f32[]{:T(128)}) all-reduce(f32[]{:T(128)} %get-tuple-element.8, f32[]{:T(128)} %get-tuple-element.9), channel_id=1, replica_groups=mesh['rows_0'=4,'rows_1'=4,'trees_0'=4,'trees_1'=2] {'trees_1'}, use_global_device_ids=true, to_apply=%region_14.15 | all-reduce | flops 2 | bytes 16 | tf_op jit(solution)/shard_map/psum | solution.py:27
  (1 shorter events, 0.0 us)
Async XLA Ops:
  7.2 181.7 %reduce-scatter.2.cloned.1.call-start = ((), (), s32[]{:S(2)}) async-start(), calls=%async_computation.2 | async-start | bytes 17825792 | tf_op jit(solution)/shard_map/reduce_scatter | solution.py:53
Sparse Core Ops, SparseCore 0:
  74.9 113.8 reduce-scatter.1
where the time goes:
time: 256 us; the launch traced here: 255 us
  waiting for transfers between devices  114 us (45%)
  blocking collectives  53.4 us (21%)
  local copies, waits for them, and re-layouts  46.7 us (18%)
  matrix products  21.7 us (8%)
  between operations  16.4 us (6%)
    reduce_scatter x1, waiting for transfers between devices, per_device(): lax.psum_scatter(ordered, ROWS, scatter_dimension=0, tiled=True)  114 us
    psum x4, blocking collectives, by_axis(): shard = lax.psum(shard, axis)  33.3 us
    dot_general x1, local copies, waits for them, and re-layouts, count_table(): jnp.einsum('rtlz,zc->rtlc', placed, class_onehot, preferred_element_type=...  25.1 us
    dot_general x1, matrix products, count_table(): jnp.einsum('rtlz,zc->rtlc', placed, class_onehot, preferred_element_type=...  21.7 us
    reshape x1, local copies, waits for them, and re-layouts, count_table(): return count_grid.reshape(-1, CLASSES)  20.8 us
    all_to_all x1, blocking collectives, summed_on_arrival(): parts = lax.all_to_all(in_blocks(shard, dim, peers), axis, 0, 0, tiled=True)  20.1 us
  transfers between devices with their start and end apart: 1, of which 1 were waited for; matrix products, arithmetic and copies ran while one was open for 0% of the time, Pallas kernels for 0%

commit v1 on v0

--- a/solution.py
+++ b/solution.py
@@ -24,7 +24,8 @@
 
 def by_axis(shard, axes):
     for axis in axes:
-        shard = lax.psum(shard, axis)
+        terms = lax.all_gather(shard, axis, axis=0, tiled=False)
+        shard = terms.sum(axis=0)
     return shard
 
 

time: 256 us -> 271 us (1.059)
  blocking collectives: 53.4 us -> 30.6 us
  local copies, waits for them, and re-layouts: 46.7 us -> 61.5 us
  waiting for transfers between devices: 114 us -> 125 us
  starting transfers between devices: 0.04 us -> 5.2 us
  other arithmetic: 2.27 us -> 7.24 us
    psum x4 -> x0, blocking collectives: 33.3 us -> none  [by_axis(): shard = lax.psum(shard, axis)]
    unnamed x0 -> x4, blocking collectives: none -> 30.6 us
    all_to_all x1 -> x0, blocking collectives: 20.1 us -> none  [summed_on_arrival(): parts = lax.all_to_all(in_blocks(shard, dim, peers), axis, 0, 0, tiled=True)]
    unnamed x0 -> x36, local copies, waits for them, and re-layouts: none -> 14.5 us
    all_to_all x0 -> x1, waiting for transfers between devices: none -> 11.2 us  [summed_on_arrival(): parts = lax.all_to_all(in_blocks(shard, dim, peers), axis, 0, 0, tiled=True)]
    all_to_all x0 -> x1, starting transfers between devices: none -> 5.16 us  [summed_on_arrival(): parts = lax.all_to_all(in_blocks(shard, dim, peers), axis, 0, 0, tiled=True)]
    reduce_sum x0 -> x12, other arithmetic: none -> 4.89 us  [by_axis(): shard = terms.sum(axis=0)]
  transfers between devices with their start and end apart: 1 -> 2, of which waited for: 1 -> 2; matrix products, arithmetic and copies ran while one was open for 0% -> 1% of each run, Pallas kernels for 0% -> 0%
where the time goes in v1:
time: 271 us; the launch traced here: 269 us
  waiting for transfers between devices  125 us (46%)
  local copies, waits for them, and re-layouts  61.5 us (23%)
  blocking collectives  30.6 us (11%)
  matrix products  21.7 us (8%)
  between operations  17.9 us (7%)
  other arithmetic  7.24 us (3%)
  starting transfers between devices  5.2 us (2%)
    reduce_scatter x1, waiting for transfers between devices, per_device(): lax.psum_scatter(ordered, ROWS, scatter_dimension=0, tiled=True)  114 us
    unnamed x4, blocking collectives  30.6 us
    dot_general x1, local copies, waits for them, and re-layouts, count_table(): jnp.einsum('rtlz,zc->rtlc', placed, class_onehot, preferred_element_type=...  25.1 us
    dot_general x1, matrix products, count_table(): jnp.einsum('rtlz,zc->rtlc', placed, class_onehot, preferred_element_type=...  21.7 us
    reshape x1, local copies, waits for them, and re-layouts, count_table(): return count_grid.reshape(-1, CLASSES)  20.8 us
    unnamed x36, local copies, waits for them, and re-layouts  14.5 us
    all_to_all x1, waiting for transfers between devices, summed_on_arrival(): parts = lax.all_to_all(in_blocks(shard, dim, peers), axis, 0, 0, tiled=True)  11.2 us
  transfers between devices with their start and end apart: 2, of which 2 were waited for; matrix products, arithmetic and copies ran while one was open for 1% of the time, Pallas kernels for 0%

profile of v1, /device:TPU:1, one launch (start us, length us, event | category | flops | bytes accessed | tf_op | source)
XLA Modules:
  0.0 269.4 jit_solution(9729830474851254904)
XLA Ops:
  7.2 21.7 %fusion = f32[16,128,2,1000]{1,3,2,0:T(8,128)} fusion(s32[16,2]{1,0:T(8,128)S(1)} %multiply_add_fusion, s32[128,2048]{1,0:T(8,128)} %param.3, bf16[128,2048]{1,0:T(8,128)(2,1)} %param.4, s32[2048]{0:T(1024)} %param.5), kind=kOutput, calls=%fused_computation.1 | convolution fusion | flops 16796041216 | bytes 17965184 | tf_op jit(solution)/shard_map/rtlz,zc->rtlc/dot_general | solution.py:42
  29.0 25.1 %copy.6 = f32[16,128,2,1000]{3,2,1,0:T(2,128)} copy(f32[16,128,2,1000]{1,3,2,0:T(8,128)} %fusion) | data formatting | bytes 32768000 | tf_op jit(solution)/shard_map/rtlz,zc->rtlc/dot_general | solution.py:42
  54.0 20.8 %reshape.34 = f32[4096,1000]{1,0:T(8,128)} reshape(f32[16,128,2,1000]{3,2,1,0:T(2,128)} %copy.6) | data formatting | bytes 32768000 | tf_op jit(solution)/shard_map/reshape | solution.py:45
  74.8 114.0 %reduce-scatter.2.cloned.1.call-done = f32[256,1000]{1,0:T(8,128)} async-done(((f32[4096,1000]{1,0:T(8,128)}), f32[256,1000]{1,0:T(8,128)}) %reduce-scatter.2.cloned.1.call-update) | async-done | bytes 1024016 | tf_op jit(solution)/shard_map/reduce_scatter | solution.py:54
  188.9 5.2 %all-to-all-start = ((f32[8,32,1000]{2,1,0:T(8,128)}), f32[8,32,1000]{2,1,0:T(8,128)S(1)}, u32[]{:S(2)}, u32[]{:S(2)}) async-start(f32[8,32,1000]{2,1,0:T(8,128)} %bitcast.20), calls=%async_computation.1 | async-start | bytes 2097152 | tf_op jit(solution)/shard_map/all_to_all | solution.py:21
  194.6 0.7 dynamic-slice.1
  197.2 0.6 dynamic-slice.7
  197.8 11.2 %all-to-all-done = f32[8,32,1000]{2,1,0:T(8,128)S(1)} async-done(((f32[8,32,1000]{2,1,0:T(8,128)}), f32[8,32,1000]{2,1,0:T(8,128)S(1)}, u32[]{:S(2)}, u32[]{:S(2)}) %all-to-all-start) | async-done | bytes 1024032 | tf_op jit(solution)/shard_map/all_to_all | solution.py:21
  209.0 0.9 fusion.9
  210.2 0.7 subtract_reduce_fusion.1
  210.9 0.7 reshape.36
  212.2 1.4 dynamic-update-slice.4
  213.6 1.4 dynamic-update-slice.8
  215.0 8.0 %all-reduce.14 = (f32[64]{0:T(128)S(1)}, f32[64]{0:T(128)S(1)}, f32[4]{0:T(128)S(1)}, f32[4]{0:T(128)S(1)}) all-reduce(f32[64]{0:T(128)S(1)} %dynamic-update-slice, f32[64]{0:T(128)S(1)} %dynamic-update-slice.2, f32[4]{0:T(128)S(1)} %dynamic-update-slice.4, ...), channel_id=2, replica_groups=mesh['rows_0'=4,'rows_1'=4,'trees_0'=4,'trees_1'=2] {'rows_0'}, use_global_device_ids=true, to_apply=%add | all-reduce | flops 136 | bytes 1088
  224.9 1.4 dynamic-update-slice.5
  226.4 1.4 dynamic-update-slice.9
  227.8 6.7 %all-reduce.13 = (f32[64]{0:T(128)S(1)}, f32[64]{0:T(128)S(1)}, f32[4]{0:T(128)S(1)}, f32[4]{0:T(128)S(1)}) all-reduce(f32[64]{0:T(128)S(1)} %dynamic-update-slice.1, f32[64]{0:T(128)S(1)} %dynamic-update-slice.3, f32[4]{0:T(128)S(1)} %dynamic-update-slice.5, ...), channel_id=3, replica_groups=mesh['rows_0'=4,'rows_1'=4,'trees_0'=4,'trees_1'=2] {'rows_1'}, use_global_device_ids=true, to_apply=%add.1 | all-reduce | flops 136 | bytes 1088
  234.5 0.6 reduce_sum.180
  235.7 1.3 dynamic-update-slice.10
  237.0 1.3 dynamic-update-slice.6
  238.4 6.9 %all-reduce.12 = (f32[4]{0:T(128)S(1)}, f32[4]{0:T(128)S(1)}) all-reduce(f32[4]{0:T(128)S(1)} %dynamic-update-slice.6, f32[4]{0:T(128)S(1)} %dynamic-update-slice.10), channel_id=1, replica_groups=mesh['rows_0'=4,'rows_1'=4,'trees_0'=4,'trees_1'=2] {'trees_0'}, use_global_device_ids=true, to_apply=%add.6 | all-reduce | flops 8 | bytes 64
  246.5 1.4 dynamic-update-slice.11
  247.9 1.4 dynamic-update-slice.7
  249.3 9.0 %all-reduce.15 = (f32[2]{0:T(128)S(1)}, f32[2]{0:T(128)S(1)}) all-reduce(f32[2]{0:T(128)S(1)} %dynamic-update-slice.7, f32[2]{0:T(128)S(1)} %dynamic-update-slice.11), channel_id=1, replica_groups=mesh['rows_0'=4,'rows_1'=4,'trees_0'=4,'trees_1'=2] {'trees_1'}, use_global_device_ids=true, to_apply=%add.7 | all-reduce | flops 4 | bytes 32
  (49 shorter events, 7.7 us)
Async XLA Ops:
  7.2 181.7 %reduce-scatter.2.cloned.1.call-start = ((), (), s32[]{:S(2)}) async-start(), calls=%async_computation.2 | async-start | bytes 17825792 | tf_op jit(solution)/shard_map/reduce_scatter | solution.py:54
  74.8 119.2 %copy-start.3 = (u32[128]{0:T(128)S(1)}, u32[128]{0:T(128)}, u32[]{:S(2)}) copy-start(u32[128]{0:T(128)} %constant.12) | copy-start | bytes 1540
  74.8 119.8 %copy-start.2 = (u32[128]{0:T(128)S(1)}, u32[128]{0:T(128)}, u32[]{:S(2)}) copy-start(u32[128]{0:T(128)} %constant.17) | copy-start | bytes 1540
  74.8 121.8 %copy-start.1 = (u32[128]{0:T(128)S(1)}, u32[128]{0:T(128)}, u32[]{:S(2)}) copy-start(u32[128]{0:T(128)} %constant.42) | copy-start | bytes 1540
  74.8 122.4 %copy-start = (u32[128]{0:T(128)S(1)}, u32[128]{0:T(128)}, u32[]{:S(2)}) copy-start(u32[128]{0:T(128)} %constant.47) | copy-start | bytes 1540
  188.9 20.1 %all-to-all-start = ((f32[8,32,1000]{2,1,0:T(8,128)}), f32[8,32,1000]{2,1,0:T(8,128)S(1)}, u32[]{:S(2)}, u32[]{:S(2)}) async-start(f32[8,32,1000]{2,1,0:T(8,128)} %bitcast.20), calls=%async_computation.1 | async-start | bytes 2097152 | tf_op jit(solution)/shard_map/all_to_all | solution.py:21
Sparse Core Ops, SparseCore 0:
  75.0 113.8 reduce-scatter.1
